TPU v7x, 32 devices: a whole 2x2x4 slice. The times are simulated.
32 devices in a mesh: gx: 4 (over z), gy: 2 (over y), gz: 4 (over x, core).
Axes of the slice: x: 2, y: 2, z: 4, core: 2. Of those that a mesh axis runs over, the one named last changes fastest.
Arguments:
- right_side: float32 [256, 128, 256], P('gx', 'gy', 'gz'), may hold values from -6 to 6
- guess: float32 [256, 128, 256], P('gx', 'gy', 'gz'), may hold values from -6 to 6
Outputs:
- solution: float32 [256, 128, 256], P('gx', 'gy', 'gz')
- residual: float32 [256, 128, 256], P('gx', 'gy', 'gz')
All inputs are finite; a program needn't handle non-finite values.
Results may differ from a plain program's by a relative error of at most 0.0003.
Values sent between devices are 32-bit elements.
A program may use at most 256 MiB of HBM per device.

v0:
```python
import jax
import jax.numpy as jnp
from jax import lax
from jax.sharding import PartitionSpec as P

LEVELS = 7
COARSE_SWEEPS = 4


def padded_2(value, sides, width, wrap):
    for axis, dim in sides:
        count, length = lax.axis_size(axis), value.shape[dim]
        up = [(i, (i + 1) % count) for i in range(count if wrap else count - 1)]
        down = [(j, i) for i, j in up]
        last = lax.slice_in_dim(value, length - width, length, axis=dim)
        leading = lax.slice_in_dim(value, 0, width, axis=dim)
        before = lax.ppermute(last, axis, up)
        after = lax.ppermute(leading, axis, down)
        value = jnp.concatenate([before, value, after], axis=dim)
    return value


def face_total(padded):
    total = padded[2:, 1:-1, 1:-1] + padded[:-2, 1:-1, 1:-1]
    total = total + padded[1:-1, 2:, 1:-1] + padded[1:-1, :-2, 1:-1]
    total = total + padded[1:-1, 1:-1, 2:] + padded[1:-1, 1:-1, :-2]
    return total


def walls(index, total):
    return (index == 0).astype(jnp.float32) + (index == total - 1).astype(jnp.float32)


def frame(offsets, block, totals):
    first = (offsets[0] + lax.iota(jnp.int32, block[0]))[:, None, None]
    second = (offsets[1] + lax.iota(jnp.int32, block[1]))[None, :, None]
    third = (offsets[2] + lax.iota(jnp.int32, block[2]))[None, None, :]
    parity = (first + second + third) % 2
    diagonal = 6.0 + walls(first, totals[0]) + walls(second, totals[1]) + walls(third, totals[2])
    return (parity == 0, parity == 1, diagonal)


def level_frame(places, counts, size):
    offsets = tuple((place * size for place in places))
    totals = tuple((count * size for count in counts))
    return frame(offsets, (size, size, size), totals)


def relax(padded, source, colour, diagonal, scale):
    updated = (scale * source + face_total(padded)) / diagonal
    return jnp.where(colour, updated, padded[1:-1, 1:-1, 1:-1])


def residual_on(padded, source, diagonal, inverse):
    return source - (diagonal * padded[1:-1, 1:-1, 1:-1] - face_total(padded)) * inverse


def restrict(remainder):
    shape = remainder.shape
    grouped = remainder.reshape(shape[0] // 2, 2, shape[1] // 2, 2, shape[2] // 2, 2)
    return jnp.sum(grouped, axis=(1, 3, 5)) * 0.125


def odd_pad(field):
    for axis in range(3):
        count = field.shape[axis]
        lowest = -lax.slice_in_dim(field, 0, 1, axis=axis)
        highest = -lax.slice_in_dim(field, count - 1, count, axis=axis)
        field = jnp.concatenate([lowest, field, highest], axis=axis)
    return field


def prolong(padded):
    centre = padded[1:-1, 1:-1, 1:-1]
    below_first = 0.25 * (padded[:-2, 1:-1, 1:-1] - centre)
    above_first = 0.25 * (padded[2:, 1:-1, 1:-1] - centre)
    below_second = 0.25 * (padded[1:-1, :-2, 1:-1] - centre)
    above_second = 0.25 * (padded[1:-1, 2:, 1:-1] - centre)
    below_third = 0.25 * (padded[1:-1, 1:-1, :-2] - centre)
    above_third = 0.25 * (padded[1:-1, 1:-1, 2:] - centre)
    along_first = jnp.stack([below_first, above_first], axis=1)[:, :, :, None, :, None]
    along_second = jnp.stack([below_second, above_second], axis=2)[:, None, :, :, :, None]
    along_third = jnp.stack([below_third, above_third], axis=3)[:, None, :, None, :, :]
    fine = centre[:, None, :, None, :, None] + along_first + along_second + along_third
    shape = centre.shape
    return fine.reshape(2 * shape[0], 2 * shape[1], 2 * shape[2])


def down_halo(field):
    return padded_2(field, (("gx", 0), ("gy", 1), ("gz", 2)), 1, False)


def up_halo(field):
    return padded_2(field, (("gx", 0), ("gy", 1), ("gz", 2)), 1, False)


def lift_halo(field):
    return padded_2(field, (("gx", 0), ("gy", 1), ("gz", 2)), 1, False)


def pad_zero(field):
    return jnp.pad(field, 1)


def reflect(padded, axis, lowest, highest):
    moved = jnp.moveaxis(padded, axis, 0)
    moved = moved.at[0].set(jnp.where(lowest, -moved[1], moved[0]))
    moved = moved.at[-1].set(jnp.where(highest, -moved[-2], moved[-1]))
    return jnp.moveaxis(moved, 0, axis)


def reflect_all(padded, places, counts):
    for axis in range(3):
        padded = reflect(padded, axis, places[axis] == 0, places[axis] == counts[axis] - 1)
    return padded


def descend(field, source, level, geometry):
    red, black, diagonal = geometry
    scale = 4.0**level
    if level == 0:
        first = relax(down_halo(field), source, red, diagonal, scale)
    else:
        first = jnp.where(red, scale * source / diagonal, 0.0)
    second = relax(down_halo(first), source, black, diagonal, scale)
    remainder = residual_on(down_halo(second), source, diagonal, 0.25**level)
    return (second, restrict(remainder))


def ascend(smoothed, source, padded, level, geometry):
    red, black, diagonal = geometry
    scale = 4.0**level
    fine = smoothed + prolong(padded)
    first = relax(up_halo(fine), source, red, diagonal, scale)
    return relax(up_halo(first), source, black, diagonal, scale)


def bottom_sweeps(source, geometry, scale, widen):
    red, black, diagonal = geometry
    field = jnp.where(red, scale * source / diagonal, 0.0)
    field = relax(widen(field), source, black, diagonal, scale)
    for sweep_index in range(COARSE_SWEEPS - 1):
        field = relax(widen(field), source, red, diagonal, scale)
        field = relax(widen(field), source, black, diagonal, scale)
    return field


def collect(source, counts):
    block = source.shape
    whole = lax.all_gather(source.reshape(1, -1), ("gx", "gy", "gz"), axis=0, tiled=True)
    grid = whole.reshape(counts + block)
    grid = jnp.transpose(grid, (0, 3, 1, 4, 2, 5))
    return grid.reshape(counts[0] * block[0], counts[1] * block[1], counts[2] * block[2])


def bottom(source, places, counts):
    scale = 4.0 ** (LEVELS - 1)
    size = source.shape[0]
    whole = collect(source, counts)
    correction = bottom_sweeps(whole, frame((0, 0, 0), whole.shape, whole.shape), scale, pad_zero)
    starts = (places[0] * size, places[1] * size, places[2] * size)
    padded = lax.dynamic_slice(odd_pad(correction), starts, (size + 2, size + 2, size + 2))
    return padded


def per_device(right_side, guess):
    counts = (lax.axis_size("gx"), lax.axis_size("gy"), lax.axis_size("gz"))
    places = (lax.axis_index("gx"), lax.axis_index("gy"), lax.axis_index("gz"))
    block = right_side.shape[0]
    frames = [level_frame(places, counts, block >> level) for level in range(LEVELS - 1)]
    field = guess
    source = right_side
    sources = []
    kept = []
    for level in range(LEVELS - 1):
        smoothed, coarse = descend(field, source, level, frames[level])
        sources.append(source)
        kept.append(smoothed)
        field = coarse
        source = coarse
    padded = bottom(source, places, counts)
    fine = guess
    for level in reversed(range(LEVELS - 1)):
        fine = ascend(kept[level], sources[level], padded, level, frames[level])
        if level > 0:
            padded = reflect_all(lift_halo(fine), places, counts)
    red, black, diagonal = frames[0]
    return (fine, residual_on(up_halo(fine), right_side, diagonal, 1.0))


def solution(mesh):
    return jax.shard_map(
        per_device,
        mesh=mesh,
        in_specs=(P("gx", "gy", "gz"), P("gx", "gy", "gz")),
        out_specs=(P("gx", "gy", "gz"), P("gx", "gy", "gz")),
        check_vma=False,
    )
```

profile of v0, /device:TPU:1, one launch (start us, length us, event | category | flops | bytes accessed | tf_op | source)
XLA Modules:
  0.0 1266.6 jit_solution(15486125261288893361)
XLA Ops:
  43.1 11.5 fusion.1
  92.1 13.8 %fusion.2 = f32[64,64,64]{2,1,0:T(8,128)S(1)} fusion(f32[64,64,64]{2,1,0:T(8,128)} %copy-done.6, f32[64,64,64]{2,1,0:T(8,128)S(1)} %copy-done, f32[66,66,1]{2,1,0:T(8,128)} %copy.286, f32[66,1,64]{2,1,0:T(1,128)S(1)} %collective-permute-done.8, f32[66,1,64]{2,1,0:T(1,128)S(1)} %collective-permute-done.9, f32[1,64,64]{2,1,0:T(8,128)S(1)} %collective-permute-done.6, ...), kind=kLoop, calls=%fused_computation.21 | loop fusion | flops 10485760 | bytes 3280416 | tf_op jit(solution)/shard_map/jit(_where)/select_n | solution.py:51
  145.4 15.9 %fusion.4 = f32[64,64,64]{2,1,0:T(8,128)} fusion(f32[64,64,64]{2,1,0:T(8,128)S(1)} %copy-done, f32[64,64,64]{2,1,0:T(8,128)} %copy-done.1, f32[66,66,1]{2,1,0:T(8,128)} %copy.290, f32[66,1,64]{2,1,0:T(1,128)S(1)} %collective-permute-done.14, f32[66,1,64]{2,1,0:T(1,128)S(1)} %collective-permute-done.15, f32[1,64,64]{2,1,0:T(8,128)S(1)} %collective-permute-done.12, ...), kind=kLoop, calls=%fused_computation.23 | loop fusion | flops 7077888 | bytes 3263776 | tf_op jit(solution)/shard_map/sub | solution.py:55
  161.3 71.5 %reshape.1848 = f32[32,2,32,2,32,2]{5,4,3,2,1,0:T(8,128)} reshape(f32[64,64,64]{2,1,0:T(8,128)} %fusion.4) | data formatting | bytes 2097152 | tf_op jit(solution)/shard_map/reshape | solution.py:60
  232.7 20.8 %reduce_sum.54 = f32[32,32,32]{2,1,0:T(8,128)S(1)} reduce(f32[32,2,32,2,32,2]{5,4,3,2,1,0:T(8,128)} %reshape.1848, f32[]{:T(128)} %constant.831.clone.1), dimensions={1,3,5}, to_apply=%region_0.1 | reduce | flops 229376 | bytes 1179652 | tf_op jit(solution)/shard_map/reduce_sum | solution.py:61
  320.4 7.1 reshape.1849
  370.0 7.4 collective-permute-start.41
  399.2 7.3 collective-permute-start.47
  424.7 7.3 collective-permute-start.53
  452.8 7.3 collective-permute-start.59
  476.5 7.2 collective-permute-start.65
  501.7 7.2 collective-permute-start.71
  534.2 36.9 %all-reduce.7 = f32[32]{0:T(128)S(1)} all-reduce(f32[32]{0:T(128)S(1)} %dynamic-update-slice.90), channel_id=1, replica_groups=mesh['gx'=4,'gy'=2,'gz'=4] {'gx','gy','gz'}, use_global_device_ids=true, to_apply=%add.7 | all-reduce | flops 32 | bytes 256
  792.8 7.1 collective-permute-start.130
  854.7 7.3 collective-permute-start.143
  877.2 7.3 collective-permute-start.148
  911.4 7.1 add.2504
  1015.0 7.2 scatter.149
  1026.2 9.4 copy.325
  1038.4 27.0 %broadcast_add_fusion = f32[32,2,32,2,32,2]{5,4,3,2,1,0:T(8,128)} fusion(f32[32,32,32,2]{3,2,1,0:T(8,128)} %copy.325, f32[32,2,32,2,32]{4,3,2,1,0:T(2,128)S(1)} %broadcast_add_fusion.2), kind=kLoop, calls=%fused_computation | loop fusion | flops 262144 | bytes 1835008 | tf_op jit(solution)/shard_map/add | solution.py:84
  1065.4 54.9 %add.2526 = f32[64,64,64]{2,1,0:T(8,128)} reshape(f32[32,2,32,2,32,2]{5,4,3,2,1,0:T(8,128)} %broadcast_add_fusion) | data formatting | bytes 2097152 | tf_op jit(solution)/shard_map/add | solution.py:84
  1155.6 13.8 %fusion.5 = f32[64,64,64]{2,1,0:T(8,128)S(1)} fusion(f32[64,64,64]{2,1,0:T(8,128)} %copy-done.5, f32[64,64,64]{2,1,0:T(8,128)S(1)} %copy-done, f32[66,66,1]{2,1,0:T(8,128)} %copy.329, f32[66,1,64]{2,1,0:T(1,128)S(1)} %collective-permute-done.170, f32[66,1,64]{2,1,0:T(1,128)S(1)} %collective-permute-done.171, f32[1,64,64]{2,1,0:T(8,128)S(1)} %collective-permute-done.168, ...), kind=kLoop, calls=%fused_computation.24 | loop fusion | flops 10485760 | bytes 3280416 | tf_op jit(solution)/shard_map/jit(_where)/select_n | solution.py:51
  1202.4 13.8 %fusion.6 = f32[64,64,64]{2,1,0:T(8,128)S(1)} fusion(f32[64,64,64]{2,1,0:T(8,128)} %copy-done.4, f32[64,64,64]{2,1,0:T(8,128)S(1)} %copy-done, f32[66,66,1]{2,1,0:T(8,128)} %copy.333, f32[66,1,64]{2,1,0:T(1,128)S(1)} %collective-permute-done.176, f32[66,1,64]{2,1,0:T(1,128)S(1)} %collective-permute-done.177, f32[1,64,64]{2,1,0:T(8,128)S(1)} %collective-permute-done.174, ...), kind=kLoop, calls=%fused_computation.25 | loop fusion | flops 10485760 | bytes 3280416 | tf_op jit(solution)/shard_map/jit(_where)/select_n | solution.py:51
  1249.7 16.4 %fusion.8 = f32[64,64,64]{2,1,0:T(8,128)} fusion(f32[64,64,64]{2,1,0:T(8,128)S(1)} %copy-done, f32[64,64,64]{2,1,0:T(8,128)} %copy-done.3, f32[66,66,1]{2,1,0:T(8,128)} %copy.337, f32[66,1,64]{2,1,0:T(1,128)S(1)} %collective-permute-done.182, f32[66,1,64]{2,1,0:T(1,128)S(1)} %collective-permute-done.183, f32[1,64,64]{2,1,0:T(8,128)S(1)} %collective-permute-done.180, ...), kind=kLoop, calls=%fused_computation.27 | loop fusion | flops 7077888 | bytes 3263776 | tf_op jit(solution)/shard_map/sub | solution.py:55
  (842 shorter events, 861.6 us)
Async XLA Ops:
  1.4 9.6 collective-permute-start
  27.5 13.3 %collective-permute-start.5 = (f32[66,66,1]{1,2,0:T(1,128)S(1)}, f32[66,66,1]{1,2,0:T(1,128)S(1)}, u32[]{:S(2)}, u32[]{:S(2)}) collective-permute-start(f32[66,66,1]{1,2,0:T(1,128)S(1)} %copy.281), channel_id=1, source_target_pairs={{0,1},{1,2},{2,3},{4,5},{5,6},{6,7},{8,9},{9,10},{10,11},{12,13},{... | collective-permute-start | bytes 52280 | tf_op jit(solution)/shard_map/ppermute | solution.py:17
  78.0 11.8 collective-permute-start.11
  131.3 11.8 collective-permute-start.17
  272.2 10.6 collective-permute-start.23
  305.3 11.1 collective-permute-start.29
  368.1 11.0 collective-permute-start.40
  370.0 10.2 collective-permute-start.41
  397.3 9.8 collective-permute-start.46
  422.8 9.7 collective-permute-start.52
  450.9 9.2 collective-permute-start.58
  474.6 9.1 collective-permute-start.64
  499.8 9.1 collective-permute-start.70
  602.8 9.3 collective-permute-start.82
  694.1 9.0 collective-permute-start.106
  716.6 9.0 collective-permute-start.112
  792.8 9.1 collective-permute-start.130
  852.8 10.9 collective-permute-start.142
  854.7 10.1 collective-permute-start.143
  877.2 10.1 collective-permute-start.148
  963.4 10.0 collective-permute-start.160
  1141.8 9.2 collective-permute-start.172
  1187.8 9.9 collective-permute-start.178
  1234.5 10.5 collective-permute-start.184
  (213 other events, 2995.6 us)
where the time goes:
time: 1280 us; the launch traced here: 1270 us
  starting transfers between devices  439 us (34%)
  local copies, waits for them, and re-layouts  304 us (24%)
  waiting for transfers between devices  246 us (19%)
  other arithmetic  227 us (18%)
  blocking collectives  36.9 us (3%)
    ppermute x93, starting transfers between devices, padded_2(): before = lax.ppermute(last, axis, up)  285 us
    ppermute x93, waiting for transfers between devices, padded_2(): after = lax.ppermute(leading, axis, down)  229 us
    ppermute x93, starting transfers between devices, padded_2(): after = lax.ppermute(leading, axis, down)  155 us
    reshape x5, local copies, waits for them, and re-layouts, restrict(): remainder.reshape(shape[0] // 2, 2, shape[1] // 2, 2, shape[2] // 2, 2)  82.9 us
    select_n x26, other arithmetic, relax(): return jnp.where(colour, updated, padded[1:-1, 1:-1, 1:-1])  80.8 us
    add x5, local copies, waits for them, and re-layouts, prolong(): centre[:, None, :, None, :, None] + along_first + along_second + along_third  65.9 us
    slice x38, local copies, waits for them, and re-layouts, padded_2(): leading = lax.slice_in_dim(value, 0, width, axis=dim)  49.4 us
    add x13, other arithmetic, prolong(): centre[:, None, :, None, :, None] + along_first + along_second + along_third  43.7 us
  transfers between devices with their start and end apart: 186, of which 95 were waited for; matrix products, arithmetic and copies ran while one was open for 3% of the time, Pallas kernels for 0%

commit v1 on v0

v1 whole, which is shorter than its diff:
```python
import jax
import jax.numpy as jnp
from jax import lax
from jax.experimental import pallas as pl
from jax.experimental.pallas import tpu as pltpu
from jax.sharding import PartitionSpec as P

LEVELS = 7
COARSE_SWEEPS = 4
GATHER = 3
LANES = 128
AXES = ("gx", "gy", "gz")
HIGHEST = lax.Precision.HIGHEST


def rows_of(count):
    return max(8, count)


def lane_iota(rows):
    return lax.broadcasted_iota(jnp.int32, (rows, LANES), 1)


def row_iota(rows):
    return lax.broadcasted_iota(jnp.int32, (rows, LANES), 0)


def loop(count, body):
    if count == 1:
        body(0)
    else:
        def step(i, carry):
            body(i)
            return carry
        lax.fori_loop(0, count, step, 0)


class Level:
    def __init__(self, number, dims, places, counts, v, s, w, d):
        self.number, self.dims, self.places, self.counts = number, dims, places, counts
        self.v, self.s, self.w, self.d = v, s, w, d
        self.rows = rows_of(dims[1])
        self.scale = 4.0 ** number
        self.inverse = 0.25 ** number
        self.chunk = min(dims[0], max(2, 32 * 8 // self.rows))

    def prepare(self):
        x, y, z = self.dims
        row, lane = row_iota(self.rows), lane_iota(self.rows)
        valid = (row < y) & (lane < z)
        at_y, at_z = self.places[1] * y + row, self.places[2] * z + lane
        one = lambda at, total: (at == 0).astype(jnp.float32) + (at == total - 1).astype(jnp.float32)
        base = 6.0 + one(at_y, self.counts[1] * y) + one(at_z, self.counts[2] * z)
        for wall in range(2):
            self.d[wall] = jnp.where(valid, base + wall, 0.0)
            for parity in range(2):
                self.w[2 * wall + parity] = jnp.where(valid & ((row + lane) % 2 == parity), 1.0 / (base + wall), 0.0)
        self.v[...] = jnp.zeros_like(self.v)

    def wall(self, plane):
        at = self.places[0] * self.dims[0] + plane
        last = self.counts[0] * self.dims[0] - 1
        if isinstance(at, int):
            return int(at in (0, last))
        return jnp.where((at == 0) | (at == last), 1, 0)

    def total(self, start, face):
        count, rows, z = self.chunk, self.rows, self.dims[2]
        slab = self.v[pl.ds(start, count + 2), pl.ds(8, rows), :]
        centre = slab[1:-1]
        total = slab[2:] + slab[:-2]
        total = total + self.v[pl.ds(start + 1, count), pl.ds(9, rows), :] + self.v[pl.ds(start + 1, count), pl.ds(7, rows), :]
        lane = lane_iota(rows)
        out = []
        for i in range(count):
            c = centre[i]
            if face is None:
                z_sum = pltpu.roll(c, 1, 1) + pltpu.roll(c, LANES - 1, 1)
            else:
                g = pltpu.roll(face[...], LANES - (start + i), 1)
                if z != 64:
                    g_high = pltpu.roll(g, LANES + z - 64, 1) if z < 64 else g
                    high = jnp.where(lane == z, g_high, c)
                else:
                    high = jnp.where(lane == 64, g, c)
                z_sum = jnp.where(lane == 0, g, pltpu.roll(c, 1, 1)) + pltpu.roll(high, LANES - 1, 1)
            out.append(total[i] + z_sum)
        return out, [centre[i] for i in range(count)]

    def sweep(self, colour, face=None, zero=False):
        def body(step):
            start = step * self.chunk
            if not zero:
                totals, centres = self.total(start, face)
            results = []
            for i in range(self.chunk):
                weight = self.w[2 * self.wall(start + i) + (i + colour) % 2]
                given = self.scale * self.s[start + i]
                if zero:
                    results.append(given * weight)
                else:
                    results.append(jnp.where(weight > 0, (given + totals[i]) * weight, centres[i]))
            for i in range(self.chunk):
                self.v[start + i + 1, pl.ds(8, self.rows), :] = results[i]
        loop(self.dims[0] // self.chunk, body)

    def remainder(self, start, face):
        totals, centres = self.total(start, face)
        out = []
        for i in range(self.chunk):
            d = self.d[self.wall(start + i)]
            out.append(jnp.where(d > 0, self.s[start + i] - (d * centres[i] - totals[i]) * self.inverse, 0.0))
        return out

    def restrict_to(self, target, pairs, face=None):
        rows, z = self.rows, self.dims[2]
        coarse_rows = rows_of(self.dims[1] // 2)
        half = self.chunk // 2
        source_lane = lax.broadcasted_iota(jnp.int32, (LANES, LANES), 0)
        target_lane = lax.broadcasted_iota(jnp.int32, (LANES, LANES), 1)
        halve = jnp.where((source_lane // 2 == target_lane) & (source_lane < z), 0.125, 0.0)
        if rows < 16:
            pairs[...] = jnp.zeros_like(pairs)

        def first(step):
            r = self.remainder(step * self.chunk, face)
            for i in range(half):
                pairs[step * half + i, pl.ds(0, rows), :] = r[2 * i] + r[2 * i + 1]
        loop(self.dims[0] // self.chunk, first)

        planes = self.dims[0] // 2
        many = min(planes, max(1, 256 // coarse_rows))

        def second(step):
            at = pl.ds(step * many, many)
            q = pairs[at, pl.ds(0, coarse_rows, stride=2), :] + pairs[at, pl.ds(1, coarse_rows, stride=2), :]
            q = jnp.dot(q.reshape(many * coarse_rows, LANES), halve, precision=HIGHEST, preferred_element_type=jnp.float32)
            target[at] = q.reshape(many, coarse_rows, LANES)
        loop(planes // many, second)

    def reflect(self):
        x, y, z = self.dims
        v = self.v

        def low_x():
            v[0] = -v[1]

        def high_x():
            v[x + 1] = -v[x]

        def low_y():
            for_all = pl.ds(1, x)
            v[for_all, pl.ds(7, 1), :] = -v[for_all, pl.ds(8, 1), :]

        def high_y():
            for_all = pl.ds(1, x)
            v[for_all, pl.ds(8 + y, 1), :] = -v[for_all, pl.ds(7 + y, 1), :]

        for axis, low, high in ((0, low_x, high_x), (1, low_y, high_y)):
            if isinstance(self.counts[axis], int) and isinstance(self.places[axis], int):
                low()
                high()
            else:
                pl.when(self.places[axis] == 0)(low)
                pl.when(self.places[axis] == self.counts[axis] - 1)(high)


def lift(v, dims, places, counts, fine, spread, high_lane, face=None):
    x, y, z = dims
    rows = rows_of(y)
    k = lax.broadcasted_iota(jnp.int32, (LANES, LANES), 0)
    f = lax.broadcasted_iota(jnp.int32, (LANES, LANES), 1)
    inside = f < 2 * z
    own = ((f // 2 == k) & inside).astype(jnp.float32)
    beside = ((f // 2 + 2 * (f % 2) - 1 == k) & inside & (k < z)).astype(jnp.float32)
    low_wall = jnp.where(places[2] == 0, 1.0, 0.0)
    high_wall = jnp.where(places[2] == counts[2] - 1, 1.0, 0.0)
    at_low, at_high = f == 0, f == 2 * z - 1
    beside = beside + jnp.where(at_low & (k == 0), -low_wall, 0.0) + jnp.where(at_low & (k == LANES - 1), 1.0 - low_wall, 0.0)
    beside = beside + jnp.where(at_high & (k == z - 1), -high_wall, 0.0) + jnp.where(at_high & (k == high_lane), 1.0 - high_wall, 0.0)
    both = 0.25 * (own + beside)
    own = 0.25 * own
    tall = rows + 16
    lane = lane_iota(rows)
    valid = row_iota(rows) < y

    def first(plane):
        spread[plane] = jnp.dot(v[plane], own, precision=HIGHEST, preferred_element_type=jnp.float32)

    group = 2
    loop((x + 2) // group, lambda step: [first(step * group + i) for i in range(group)])

    def second(plane):
        e = v[plane + 1, pl.ds(8, rows), :]
        if face is not None:
            e = jnp.where(lane < z, e, pltpu.roll(pltpu.roll(face[...], LANES - plane, 1), LANES - 1, 1))
        centre = jnp.dot(e, both, precision=HIGHEST, preferred_element_type=jnp.float32)
        ys = (spread[plane + 1, pl.ds(7, rows), :], spread[plane + 1, pl.ds(9, rows), :])
        for up_x in range(2):
            xs = centre + spread[plane + 2 * up_x, pl.ds(8, rows), :]
            for up_y in range(2):
                q = xs + ys[up_y]
                if y < rows:
                    q = jnp.where(valid, q, 0.0)
                at = (2 * plane + up_x + 1, pl.ds(8 + up_y, rows, stride=2), slice(None))
                fine.v[at] = fine.v[at] + q

    loop(x // group, lambda step: [second(step * group + i) for i in range(group)])


def solve_kernel(counts, blocks, coarse, uses, refs):
    right_side, guess, out_v, out_r = refs[:4]
    refs = list(refs[4:])
    take = lambda: refs.pop(0)
    places = tuple(lax.axis_index(axis) for axis in AXES)
    levels = []
    for number, dims in enumerate(blocks[:GATHER]):
        levels.append(Level(number, dims, places, counts, take(), take(), take(), take()))
    for number, dims in enumerate(coarse):
        levels.append(Level(GATHER + number, dims, (0, 0, 0), (1, 1, 1), take(), take(), take(), take()))
    exchange = [(take(), take(), take(), take(), take()) for _ in range(GATHER)]
    pairs = [take() for _ in range(LEVELS - 1)]
    spreads = [take() for _ in range(LEVELS - 1)]
    block_s, block_v, packet, packets, gather_send, gather_recv = refs

    for level in levels:
        level.prepare()
    for number in range(GATHER):
        exchange[number][4][...] = jnp.zeros_like(exchange[number][4])
    z0 = blocks[0][2]
    top = levels[0]

    def load(x):
        top.v[x + 1, pl.ds(8, top.rows), pl.ds(0, z0)] = guess[x]
        top.s[x] = jnp.concatenate([right_side[x], jnp.zeros((top.rows, LANES - z0), jnp.float32)], axis=1)
    loop(blocks[0][0] // 4, lambda step: [load(4 * step + i) for i in range(4)])

    turn = [0] * GATHER
    sent = []

    def swap(number):
        level = levels[number]
        out, into, send, recv, face = exchange[number]
        n, v, (x, y, z) = turn[number], level.v, level.dims
        turn[number] += 1
        out[n, 0, pl.ds(0, y)] = v[x, pl.ds(8, y), :]
        out[n, 1, pl.ds(0, y)] = v[1, pl.ds(8, y), :]
        out[n, 2, pl.ds(0, x)] = v[pl.ds(1, x), 7 + y, :]
        out[n, 3, pl.ds(0, x)] = v[pl.ds(1, x), 8, :]
        lane = lane_iota(y)
        many = min(x, 8)

        def columns(step, carry):
            last, leading = carry
            for i in range(many):
                plane = step * many + i
                c = v[plane + 1, pl.ds(8, y), :]
                last = jnp.where(lane == plane, pltpu.roll(c, plane + LANES - (z - 1), 1), last)
                leading = jnp.where(lane == plane + 64, pltpu.roll(c, plane + 64, 1), leading)
            return last, leading
        zero = jnp.zeros((y, LANES), jnp.float32)
        last, leading = lax.fori_loop(0, x // many, columns, (zero, zero))
        out[n, 4, pl.ds(0, y)] = last
        out[n, 5, pl.ds(0, y)] = leading

        copies = []
        for axis in range(3):
            for way in range(2):
                side = 2 * axis + way
                other = places[axis] + (1 - 2 * way)
                copy = pltpu.make_async_remote_copy(
                    src_ref=out.at[n, side], dst_ref=into.at[n, side],
                    send_sem=send.at[n, side], recv_sem=recv.at[n, side],
                    device_id={AXES[axis]: other}, device_id_type=pl.DeviceIdType.MESH)
                has_target = other < counts[axis] if way == 0 else other >= 0
                has_origin = places[axis] > 0 if way == 0 else places[axis] < counts[axis] - 1
                pl.when(has_target)(copy.start)
                sent.append((has_target, copy))
                copies.append((has_origin, copy))

        def land(side):
            got = into.at[n, side]
            if side == 0:
                v[0, pl.ds(8, y), :] = got[pl.ds(0, y)]
            elif side == 1:
                v[x + 1, pl.ds(8, y), :] = got[pl.ds(0, y)]
            elif side == 2:
                v[pl.ds(1, x), 7, :] = got[pl.ds(0, x)]
            elif side == 3:
                v[pl.ds(1, x), 8 + y, :] = got[pl.ds(0, x)]
            elif side == 4:
                face[...] = jnp.where(lane < 64, got[pl.ds(0, y)], face[...])
            else:
                face[...] = jnp.where(lane >= 64, got[pl.ds(0, y)], face[...])
        for side, (has_origin, copy) in enumerate(copies):
            @pl.when(has_origin)
            def _(side=side, copy=copy):
                copy.wait_recv()
                land(side)
        return face

    for number in range(GATHER):
        level = levels[number]
        if number == 0:
            level.sweep(0, swap(0))
        else:
            level.sweep(0, zero=True)
        level.sweep(1, swap(number))
        target = levels[number + 1].s if number + 1 < GATHER else block_s
        level.restrict_to(target, pairs[number], swap(number))

    bx, by, bz = blocks[GATHER]
    packed = block_s[0]
    for x in range(1, bx):
        packed = packed + pltpu.roll(block_s[x], x * bz, 1)
    packet[...] = packed
    total = counts[0] * counts[1] * counts[2]
    me = (places[0] * counts[1] + places[1]) * counts[2] + places[2]

    def gather_copy(source, target, offset):
        return pltpu.make_async_remote_copy(
            src_ref=packet, dst_ref=packets.at[source],
            send_sem=gather_send.at[target], recv_sem=gather_recv.at[source],
            device_id=(target // (counts[1] * counts[2]), target // counts[2] % counts[1], target % counts[2]),
            device_id_type=pl.DeviceIdType.MESH)

    def post(offset, carry):
        gather_copy(me, lax.rem(me + offset, total), offset).start()
        return carry
    lax.fori_loop(1, total, post, 0)
    packets[me] = packed

    def arrive(offset, carry):
        source = lax.rem(me + total - offset, total)
        gather_copy(source, lax.rem(me + offset, total), offset).wait_recv()
        return carry
    lax.fori_loop(1, total, arrive, 0)
    whole = levels[GATHER]
    lane = lane_iota(by)

    def unpack(step):
        px, py = step // counts[1], step % counts[1]
        for x in range(bx):
            row = jnp.zeros((by, LANES), jnp.float32)
            for pz in range(counts[2]):
                shifted = pltpu.roll(packets[step * counts[2] + pz], (pz * bz - x * bz) % LANES, 1)
                row = jnp.where((lane >= pz * bz) & (lane < pz * bz + bz), shifted, row)
            whole.s[px * bx + x, pl.ds(pl.multiple_of(py * by, 8), by), :] = row
    loop(counts[0] * counts[1], unpack)

    for number in range(GATHER, LEVELS - 1):
        level = levels[number]
        level.sweep(0, zero=True)
        level.sweep(1)
        level.restrict_to(levels[number + 1].s, pairs[number])
    level = levels[LEVELS - 1]
    level.sweep(0, zero=True)
    level.sweep(1)
    for _ in range(COARSE_SWEEPS - 1):
        level.sweep(0)
        level.sweep(1)
    for number in reversed(range(GATHER, LEVELS - 1)):
        level, below = levels[number], levels[number + 1]
        below.reflect()
        lift(below.v, below.dims, (0, 0, 0), (1, 1, 1), level, spreads[number], below.dims[2])
        level.sweep(0)
        level.sweep(1)

    whole.reflect()
    shift = lax.rem(LANES - places[2] * bz, LANES)
    for x in range(bx + 2):
        part = whole.v[places[0] * bx + x, pl.ds(pl.multiple_of(places[1] * by, 8), by + 16), :]
        block_v[x] = pltpu.roll(part, shift, 1)
    lift(block_v, blocks[GATHER], places, counts, levels[GATHER - 1], spreads[GATHER - 1], bz)
    for number in reversed(range(GATHER)):
        level = levels[number]
        level.sweep(0, swap(number))
        level.sweep(1, swap(number))
        face = swap(number)
        if number > 0:
            level.reflect()
            lift(level.v, level.dims, places, counts, levels[number - 1], spreads[number - 1], 63, face)

    def finish(step):
        r = top.remainder(step * top.chunk, face)
        for i in range(top.chunk):
            at = step * top.chunk + i
            out_r[at] = r[i][:, :z0]
            out_v[at] = top.v[at + 1, pl.ds(8, top.rows), pl.ds(0, z0)]
    loop(blocks[0][0] // top.chunk, finish)

    for has_target, copy in sent:
        pl.when(has_target)(copy.wait_send)

    def leave(offset, carry):
        gather_copy(me, lax.rem(me + offset, total), offset).wait_send()
        return carry
    lax.fori_loop(1, total, leave, 0)


def solution(mesh):
    counts = tuple(mesh.shape[axis] for axis in AXES)

    def per_device(right_side, guess):
        shape = right_side.shape
        blocks = [tuple(side >> level for side in shape) for level in range(GATHER + 1)]
        whole = tuple(side * count for side, count in zip(blocks[GATHER], counts))
        coarse = [tuple(side >> level for side in whole) for level in range(LEVELS - GATHER)]
        grids = blocks[:GATHER] + coarse
        scratch = []
        vmem = lambda *dims: scratch.append(pltpu.VMEM(dims, jnp.float32))
        for x, y, z in grids:
            vmem(x + 2, rows_of(y) + 16, LANES)
            vmem(x, rows_of(y), LANES)
            vmem(4, rows_of(y), LANES)
            vmem(2, rows_of(y), LANES)
        for number, (x, y, z) in enumerate(blocks[:GATHER]):
            turns = 6 if number == 0 else 5
            side = max(x, y)
            vmem(turns, 6, side, LANES)
            vmem(turns, 6, side, LANES)
            scratch.append(pltpu.SemaphoreType.DMA((turns, 6)))
            scratch.append(pltpu.SemaphoreType.DMA((turns, 6)))
            vmem(y, LANES)
        for x, y, z in grids[:-1]:
            vmem(x // 2, max(16, y), LANES)
        for number in range(LEVELS - 1):
            x, y, z = blocks[number + 1] if number < GATHER else grids[number + 1]
            vmem(x + 2, rows_of(y) + 16, LANES)
        bx, by, bz = blocks[GATHER]
        vmem(bx, by, LANES)
        vmem(bx + 2, by + 16, LANES)
        vmem(by, LANES)
        total = counts[0] * counts[1] * counts[2]
        vmem(total, by, LANES)
        scratch.append(pltpu.SemaphoreType.DMA((total,)))
        scratch.append(pltpu.SemaphoreType.DMA((total,)))

        def kernel(*refs):
            solve_kernel(counts, blocks, coarse, None, refs)

        whole_block = pl.BlockSpec(memory_space=pltpu.VMEM)
        return pl.pallas_call(
            kernel,
            out_shape=(jax.ShapeDtypeStruct(shape, jnp.float32),) * 2,
            in_specs=[whole_block] * 2,
            out_specs=(whole_block,) * 2,
            scratch_shapes=scratch,
            compiler_params=pltpu.CompilerParams(has_side_effects=True, vmem_limit_bytes=60 * 2**20),
            name="vcycle",
        )(right_side, guess)

    spec = P(*AXES)
    return jax.shard_map(per_device, mesh=mesh, in_specs=(spec, spec), out_specs=(spec, spec), check_vma=False)
```

time: 1280 us -> 139 us (0.11); the launches traced: 1270 us -> 139 us
  starting transfers between devices: 439 us -> 0 us
  local copies, waits for them, and re-layouts: 304 us -> 4.63 us
  waiting for transfers between devices: 246 us -> 0 us
  other arithmetic: 227 us -> 0 us
  Pallas kernels: 0 us -> 133 us
  blocking collectives: 36.9 us -> 0 us
    ppermute x186 -> x0, starting transfers between devices: 439 us -> none  [the longest x93 285 us: padded_2(): before = lax.ppermute(last, axis, up)]
    ppermute x186 -> x0, waiting for transfers between devices: 246 us -> none  [the longest x93 229 us: padded_2(): after = lax.ppermute(leading, axis, down)]
    pallas_call x0 -> x1, Pallas kernels: none -> 133 us  [per_device(): pl.pallas_call(kernel, out_shape=(jax.ShapeDtypeStruct(shape, jnp.float32...]
    select_n x52 -> x0, other arithmetic: 87.7 us -> none  [the longest x26 80.8 us: relax(): return jnp.where(colour, updated, padded[1:-1, 1:-1, 1:-1])]
    reshape x5 -> x0, local copies, waits for them, and re-layouts: 82.9 us -> none  [restrict(): remainder.reshape(shape[0] // 2, 2, shape[1] // 2, 2, shape[2] // 2, 2)]
    slice x91 -> x0, local copies, waits for them, and re-layouts: 72.8 us -> none  [the longest x38 49.4 us: padded_2(): leading = lax.slice_in_dim(value, 0, width, axis=dim)]
    add x5 -> x0, local copies, waits for them, and re-layouts: 65.9 us -> none  [prolong(): centre[:, None, :, None, :, None] + along_first + along_second + along_third]
    add x59 -> x0, other arithmetic: 56.6 us -> none  [the longest x13 43.7 us: prolong(): centre[:, None, :, None, :, None] + along_first + along_second + along_third]
  transfers between devices with their start and end apart: 186 -> 0, of which waited for: 95 -> 0; matrix products, arithmetic and copies ran while one was open for 3% -> 0% of each run, Pallas kernels for 0% -> 0%
where the time goes in v1:
time: 139 us
  Pallas kernels  133 us (96%)
  local copies, waits for them, and re-layouts  4.63 us (3%)
    pallas_call x1, Pallas kernels, per_device(): pl.pallas_call(kernel, out_shape=(jax.ShapeDtypeStruct(shape, jnp.float32...  133 us
    unnamed x4, local copies, waits for them, and re-layouts  4.63 us

profile of v1, /device:TPU:1, one launch (start us, length us, event | category | flops | bytes accessed | tf_op | source)
XLA Modules:
  0.0 138.5 jit_solution(16339849087421383161)
XLA Ops:
  0.6 133.3 %vcycle.1 = (f32[64,64,64]{2,1,0:T(8,128)}, f32[64,64,64]{2,1,0:T(8,128)}) custom-call(f32[64,64,64]{2,1,0:T(8,128)} %refs_0_.1, f32[64,64,64]{2,1,0:T(8,128)} %refs_1_.1), custom_call_target="tpu_custom_call" | custom-call | tf_op jit(solution)/shard_map/vcycle/pallas_call | solution.py:443
  133.9 0.0 copy-start
  133.9 3.3 %copy.6 = f32[64,64,64]{2,1,0:T(8,128)} copy(f32[64,64,64]{2,1,0:T(8,128)} %get-tuple-element.4) | data formatting | bytes 2097152
  137.2 0.0 copy-done
  137.2 1.3 copy.7
Async XLA Ops:
  133.9 3.3 %copy-start = (f32[64,64,64]{2,1,0:T(8,128)S(1)}, f32[64,64,64]{2,1,0:T(8,128)}, u32[]{:S(2)}) copy-start(f32[64,64,64]{2,1,0:T(8,128)} %get-tuple-element.5) | copy-start | bytes 3145732
